TPU v7x, 32 devices: a whole 2x2x4 slice. The times are simulated.
32 devices in a mesh: traj: 16 (over z, y, core), tm: 2 (over x).
Axes of the slice: x: 2, y: 2, z: 4, core: 2. Of those that a mesh axis runs over, the one named last changes fastest.
Arguments:
- states: float32 [2, 32, 4096], P('tm', None, 'traj'), may hold values from -6 to 6
- vectors: bfloat16 [64, 4096], P(None, 'traj'), may hold values from -6 to 6
- kernel_scale: float32 [2], P('tm'), may hold values from 6 to 16
- neighbour_blocks: int32 [32, 24], P('traj'), may hold values from 0 to 31, as said below
- neighbour_count: int32 [32], P('traj'), may hold values from 6 to 24, as said below
Outputs:
- result: float32 [64, 4096], P(None, 'traj')
Inputs may be any that keep to these rules, and one draw needn't show every extreme that they name: `neighbour_blocks`: row b names 24 different blocks, the first of them b itself. Only the first neighbour_count[b] entries of row b of neighbour_blocks are neighbours of block b; some block uses all 24.
All inputs are finite; a program needn't handle non-finite values.
Results may differ from a plain program's by a relative error of at most 0.0013.
Values may be sent and summed in bfloat16 or wider, within the bound.
No kernel may reach another device: no remote copies, remote signals or barrier semaphores. Data moves between devices by JAX's collectives and lax.ppermute only.
A program may use at most 64 MiB of HBM per device.

v0:
```python
import math
import jax
import jax.numpy as jnp
from jax import lax
from jax.sharding import PartitionSpec as P

BLK = 128


def linked_blocks(neighbour_blocks, neighbour_count, blocks_total):
    slots = neighbour_blocks.shape[1]
    named = neighbour_blocks[:, :, None] == jnp.arange(blocks_total, dtype=jnp.int32)[None, None, :]
    within = jnp.arange(slots, dtype=jnp.int32)[None, :, None] < neighbour_count[:, None, None]
    return jnp.any(named & within, axis=1).astype(jnp.float32)


def per_device(states, vectors, kernel_scale, neighbour_blocks, neighbour_count):
    coords_all = lax.all_gather(states, "traj", axis=2, tiled=True)[0]
    vectors_all = lax.all_gather(vectors, "traj", axis=1, tiled=True)
    own = states[0]
    spread = kernel_scale[0]
    own_rows = own.shape[1]
    columns = coords_all.shape[1]
    vector_count = vectors.shape[0]
    blocks_total = columns // BLK
    block_rows = own_rows // BLK
    own_squares = jnp.sum(own * own, axis=0)
    all_squares = jnp.sum(coords_all * coords_all, axis=0)
    tile_width = math.gcd(columns, 512)
    tile_count = columns // tile_width
    linked = linked_blocks(neighbour_blocks, neighbour_count, blocks_total)

    def dense_kernel(tile_index):
        offset = tile_index * tile_width
        slab = lax.dynamic_slice_in_dim(coords_all, offset, tile_width, 1)
        cross = lax.dot_general(
            own, slab, (((0,), (0,)), ((), ())), precision=lax.Precision.HIGHEST
        )
        slab_squares = lax.dynamic_slice_in_dim(all_squares, offset, tile_width, 0)
        distance = own_squares[:, None] + slab_squares[None, :] - 2.0 * cross
        mask = lax.dynamic_slice_in_dim(linked, offset // BLK, tile_width // BLK, 1)
        shaped = jnp.exp(-distance / spread).reshape(block_rows, BLK, tile_width // BLK, BLK)
        return (mask[:, None, :, None] * shaped).reshape(own_rows, tile_width)

    def first_dense(tile_index, carry):
        row_sum, pushed = carry
        kernel = dense_kernel(tile_index)
        weights = kernel.astype(jnp.bfloat16)
        slab_vectors = lax.dynamic_slice_in_dim(vectors_all, tile_index * tile_width, tile_width, 1)
        pushed = pushed + lax.dot_general(
            slab_vectors, weights, (((1,), (1,)), ((), ())), preferred_element_type=jnp.float32
        )
        return (row_sum + jnp.sum(kernel, axis=1), pushed)

    row_sum, pushed = lax.fori_loop(
        0,
        tile_count,
        first_dense,
        (jnp.zeros((own_rows,), jnp.float32), jnp.zeros((vector_count, own_rows), jnp.float32)),
    )
    scaled = (pushed / (row_sum * row_sum)[None, :]).astype(jnp.bfloat16)
    lists_whole, counts_whole = (
        lax.all_gather(neighbour_blocks, "traj", axis=0, tiled=True),
        lax.all_gather(neighbour_count, "traj", axis=0, tiled=True),
    )
    linked_whole = linked_blocks(lists_whole, counts_whole, blocks_total)
    own_start = lax.axis_index("traj") * block_rows
    column_mask = lax.dynamic_slice_in_dim(linked_whole, own_start, block_rows, 1)
    scaled_whole = lax.all_gather(scaled, "traj", axis=1, tiled=True)

    def pull_tile(tile_index, total):
        offset = tile_index * tile_width
        slab = lax.dynamic_slice_in_dim(coords_all, offset, tile_width, 1)
        cross = lax.dot_general(
            slab, own, (((0,), (0,)), ((), ())), precision=lax.Precision.HIGHEST
        )
        slab_squares = lax.dynamic_slice_in_dim(all_squares, offset, tile_width, 0)
        distance = slab_squares[:, None] + own_squares[None, :] - 2.0 * cross
        mask = lax.dynamic_slice_in_dim(column_mask, offset // BLK, tile_width // BLK, 0)
        shaped = jnp.exp(-distance / spread).reshape(tile_width // BLK, BLK, block_rows, BLK)
        weights = (
            (mask[:, None, :, None] * shaped).reshape(tile_width, own_rows).astype(jnp.bfloat16)
        )
        slab_scaled = lax.dynamic_slice_in_dim(scaled_whole, offset, tile_width, 1)
        return total + jnp.dot(slab_scaled, weights, preferred_element_type=jnp.float32)

    own_pulled = lax.fori_loop(
        0, tile_count, pull_tile, jnp.zeros((vector_count, own_rows), jnp.float32)
    )
    result = lax.psum(own_pulled, "tm")
    return result


def solution(mesh):
    in_specs = (P("tm", None, "traj"), P(None, "traj"), P("tm"), P("traj", None), P("traj"))
    out_specs = P(None, "traj")
    return jax.shard_map(
        per_device, mesh=mesh, in_specs=in_specs, out_specs=out_specs, check_vma=False
    )
```

profile of v0, /device:TPU:0, one launch (start us, length us, event | category | flops | bytes accessed | tf_op | source)
XLA Modules:
  0.0 164.4 jit_solution(14845167993915511679)
XLA Ops:
  6.5 24.9 %all_gather.15 = f32[1,32,4096]{2,1,0:T(8,128)S(1)} all-gather(f32[1,32,256]{2,1,0:T(8,128)} %param.9), channel_id=1, replica_groups=mesh['traj'=16,'tm'=2] {'traj'}, dimensions={2}, use_global_device_ids=true | all-gather | bytes 557056 | tf_op jit(solution)/shard_map/all_gather | solution.py:18
  31.6 0.7 copy-done.2
  32.3 19.0 %all_gather.16 = bf16[64,4096]{1,0:T(8,128)(2,1)S(1)} all-gather(bf16[64,256]{1,0:T(8,128)(2,1)S(1)} %copy-done.2), channel_id=1, replica_groups=mesh['traj'=16,'tm'=2] {'traj'}, dimensions={1}, use_global_device_ids=true | all-gather | bytes 557056 | tf_op jit(solution)/shard_map/all_gather | solution.py:19
  51.4 0.6 copy-done.3
  52.1 17.0 %while.34 = (s32[]{:T(128)}, f32[256]{0:T(256)S(1)}, f32[64,256]{1,0:T(8,128)S(1)}, f32[2,32]{1,0:T(2,128)S(1)}, f32[256]{0:T(256)S(1)}, /*index=5*/f32[4096]{0:...) while((s32[]{:T(128)}, f32[256]{0:T(256)S(1)}, ...), condition=%wide.region_6.7_spmd.clone, body=%wide.region_4.0_spmd.clone.sunk | while | flops 68190488 | bytes 1879617 | solution.py:55
  52.3 0.2 mul.158
  52.6 1.4 fusion.42
  54.0 0.2 convolution_add_fusion.4
  54.4 0.2 mul.158
  54.7 1.4 fusion.42
  56.1 0.2 convolution_add_fusion.4
  56.5 0.2 mul.158
  56.8 1.4 fusion.42
  58.2 0.2 convolution_add_fusion.4
  58.7 0.2 mul.158
  59.0 1.4 fusion.42
  60.4 0.2 convolution_add_fusion.4
  60.8 0.2 mul.158
  61.1 1.4 fusion.42
  62.5 0.2 convolution_add_fusion.4
  62.9 0.2 mul.158
  63.2 1.4 fusion.42
  64.6 0.2 convolution_add_fusion.4
  65.1 0.2 mul.158
  65.4 1.4 fusion.42
  66.8 0.2 convolution_add_fusion.4
  67.2 0.2 mul.158
  67.5 1.4 fusion.42
  68.9 0.2 convolution_add_fusion.4
  69.1 20.3 %all_gather.17 = bf16[64,4096]{1,0:T(8,128)(2,1)S(1)} all-gather(bf16[64,256]{1,0:T(8,128)(2,1)S(1)} %divide_convert_fusion), channel_id=1, replica_groups=mesh['traj'=16,'tm'=2] {'traj'}, dimensions={1}, use_global_device_ids=true | all-gather | bytes 557056 | tf_op jit(solution)/shard_map/all_gather | solution.py:69
  89.5 0.7 copy-done.5
  90.1 0.7 dynamic-slice
  91.5 0.2 dynamic-update-slice
  91.7 8.0 %all-reduce = s32[32]{0:T(128)S(1)} all-reduce(s32[32]{0:T(128)S(1)} %dynamic-update-slice), channel_id=1, replica_groups=mesh['traj'=16,'tm'=2] {'traj'}, use_global_device_ids=true, to_apply=%add | all-reduce | flops 32 | bytes 256
  99.8 21.6 %all-gather = s32[16,2,24]{2,1,0:T(2,128)S(1)} all-gather(s32[1,2,24]{2,1,0:T(2,128)S(1)} %bitcast.53), channel_id=1, replica_groups=mesh['traj'=16,'tm'=2] {'traj'}, dimensions={0}, use_global_device_ids=true | all-gather | bytes 3264 | tf_op jit(solution)/shard_map/all_gather | solution.py:63
  121.3 0.3 fusion.22
  121.7 15.4 %while.35 = (s32[]{:T(128)}, f32[64,256]{1,0:T(8,128)S(1)}, bf16[64,4096]{1,0:T(8,128)(2,1)S(1)}, f32[32,2]{1,0:T(8,128)S(1)}, f32[4096]{0:T(1024)S(1)}, /*index...) while((s32[]{:T(128)}, f32[64,256]{1,0:T(8,128)S(1)}, ...), condition=%wide.region_8.9_spmd.clone, body=%wide.region_7.8_spmd.clone.sunk | while | flops 68059160 | bytes 1875448 | solution.py:87
  121.7 0.2 mul.162
  122.0 1.4 fusion.47
  123.4 0.2 convolution_add_fusion.5
  123.7 0.2 mul.162
  124.0 1.4 fusion.47
  125.3 0.2 convolution_add_fusion.5
  125.6 0.2 mul.162
  125.9 1.4 fusion.47
  127.3 0.2 convolution_add_fusion.5
  127.5 0.2 mul.162
  127.8 1.4 fusion.47
  129.2 0.2 convolution_add_fusion.5
  129.5 0.2 mul.162
  129.8 1.4 fusion.47
  131.1 0.2 convolution_add_fusion.5
  131.4 0.2 mul.162
  131.7 1.4 fusion.47
  133.1 0.2 convolution_add_fusion.5
  133.3 0.2 mul.162
  133.6 1.4 fusion.47
  135.0 0.2 convolution_add_fusion.5
  135.2 0.2 mul.162
  135.5 1.4 fusion.47
  136.9 0.2 convolution_add_fusion.5
  137.1 0.6 copy-done
  137.8 18.3 %all-reduce.3.cloned.1.call-done = f32[64,256]{1,0:T(8,128)} async-done(((f32[64,256]{1,0:T(8,128)}), f32[64,256]{1,0:T(8,128)}) %all-reduce.3.cloned.1.call-update) | async-done | bytes 65552 | tf_op jit(solution)/shard_map/psum | solution.py:90
  156.1 1.5 copy.35
  (71 shorter events, 3.3 us)
Async XLA Ops:
  6.5 24.9 %copy-start.1 = (f32[1,32,256]{2,1,0:T(8,128)S(1)}, f32[1,32,256]{2,1,0:T(8,128)}, u32[]{:S(2)}) copy-start(f32[1,32,256]{2,1,0:T(8,128)} %param.9) | copy-start | bytes 98308
  6.5 149.6 %all-reduce.3.cloned.1.call-start = ((), (), s32[]{:S(2)}) async-start(), calls=%async_computation | async-start | bytes 131072 | tf_op jit(solution)/shard_map/psum | solution.py:90
  31.5 0.8 copy-start.2
  32.3 19.0 %copy-start.4 = (s32[2]{0:T(128)S(1)}, s32[2]{0:T(128)}, u32[]{:S(2)}) copy-start(s32[2]{0:T(128)} %param.13) | copy-start | bytes 28
  51.3 0.7 copy-start.3
  89.5 0.7 copy-start.5
  137.1 0.6 copy-start
Sparse Core Ops, SparseCore 0:
  137.9 18.1 all-reduce.2
where the time goes:
time: 165 us; the launch traced here: 164 us
  blocking collectives  93.8 us (57%)
  matrix products  25.1 us (15%)
  waiting for transfers between devices  18.4 us (11%)
  between operations  14.2 us (9%)
  local copies, waits for them, and re-layouts  10.9 us (7%)
    all_gather x1, blocking collectives, per_device(): coords_all = lax.all_gather(states, 'traj', axis=2, tiled=True)[0]  24.9 us
    all_gather x1, blocking collectives, per_device(): lax.all_gather(neighbour_blocks, 'traj', axis=0, tiled=True)  21.6 us
    all_gather x1, blocking collectives, per_device(): scaled_whole = lax.all_gather(scaled, 'traj', axis=1, tiled=True)  20.3 us
    all_gather x1, blocking collectives, per_device(): vectors_all = lax.all_gather(vectors, 'traj', axis=1, tiled=True)  19 us
    psum x1, waiting for transfers between devices, per_device(): result = lax.psum(own_pulled, 'tm')  18.3 us
    dot_general x8, matrix products, dense_kernel(): lax.dot_general(own, slab, (((0,), (0,)), ((), ())), precision=lax.Precis...  11.2 us
    dot_general x8, matrix products, pull_tile(): lax.dot_general(slab, own, (((0,), (0,)), ((), ())), precision=lax.Precis...  10.9 us
    unnamed x1, blocking collectives  7.97 us
  transfers between devices with their start and end apart: 1, of which 1 were waited for; matrix products, arithmetic and copies ran while one was open for 0% of the time, Pallas kernels for 0%

commit v1 on v0

--- a/solution.py
+++ b/solution.py
@@ -87,7 +87,7 @@
     own_pulled = lax.fori_loop(
         0, tile_count, pull_tile, jnp.zeros((vector_count, own_rows), jnp.float32)
     )
-    result = lax.psum(own_pulled, "tm")
+    result = jnp.sum(lax.all_gather(own_pulled, "tm"), axis=0)
     return result
 
 

time: 165 us -> 137 us (0.83)
  waiting for transfers between devices: 18.4 us -> 0 us
  between operations: 14.2 us -> 0.73 us
  blocking collectives: 93.8 us -> 98.5 us
    psum x1 -> x0, waiting for transfers between devices: 18.3 us -> none  [per_device(): result = lax.psum(own_pulled, 'tm')]
    all_gather x0 -> x1, blocking collectives: none -> 5 us  [per_device(): result = jnp.sum(lax.all_gather(own_pulled, 'tm'), axis=0)]
    unnamed x16 -> x13, local copies, waits for them, and re-layouts: 4.95 us -> 3.47 us
  transfers between devices with their start and end apart: 1 -> 0, of which waited for: 1 -> 0; matrix products, arithmetic and copies ran while one was open for 0% -> 0% of each run, Pallas kernels for 0% -> 0%
where the time goes in v1:
time: 137 us
  blocking collectives  98.5 us (72%)
  matrix products  25.1 us (18%)
  local copies, waits for them, and re-layouts  9.42 us (7%)
  other arithmetic  1.46 us (1%)
    all_gather x1, blocking collectives, per_device(): coords_all = lax.all_gather(states, 'traj', axis=2, tiled=True)[0]  24.8 us
    all_gather x1, blocking collectives, per_device(): lax.all_gather(neighbour_blocks, 'traj', axis=0, tiled=True)  21.6 us
    all_gather x1, blocking collectives, per_device(): scaled_whole = lax.all_gather(scaled, 'traj', axis=1, tiled=True)  20.3 us
    all_gather x1, blocking collectives, per_device(): vectors_all = lax.all_gather(vectors, 'traj', axis=1, tiled=True)  18.9 us
    dot_general x8, matrix products, dense_kernel(): lax.dot_general(own, slab, (((0,), (0,)), ((), ())), precision=lax.Precis...  11.2 us
    dot_general x8, matrix products, pull_tile(): lax.dot_general(slab, own, (((0,), (0,)), ((), ())), precision=lax.Precis...  10.9 us
    unnamed x1, blocking collectives  7.97 us
    all_gather x1, blocking collectives, per_device(): result = jnp.sum(lax.all_gather(own_pulled, 'tm'), axis=0)  5 us

profile of v1, /device:TPU:0, one launch (start us, length us, event | category | flops | bytes accessed | tf_op | source)
XLA Modules:
  0.0 136.5 jit_solution(8495151865991509928)
XLA Ops:
  0.0 24.8 %all_gather.21 = f32[1,32,4096]{2,1,0:T(8,128)S(1)} all-gather(f32[1,32,256]{2,1,0:T(8,128)} %param.9), channel_id=1, replica_groups=mesh['traj'=16,'tm'=2] {'traj'}, dimensions={2}, use_global_device_ids=true | all-gather | bytes 557056 | tf_op jit(solution)/shard_map/all_gather | solution.py:18
  24.9 0.7 copy-done
  25.6 18.9 %all_gather.22 = bf16[64,4096]{1,0:T(8,128)(2,1)S(1)} all-gather(bf16[64,256]{1,0:T(8,128)(2,1)S(1)} %copy-done.1), channel_id=1, replica_groups=mesh['traj'=16,'tm'=2] {'traj'}, dimensions={1}, use_global_device_ids=true | all-gather | bytes 557056 | tf_op jit(solution)/shard_map/all_gather | solution.py:19
  44.5 0.7 copy-done.3
  45.2 0.6 copy-done.2
  45.9 17.0 %while.34 = (s32[]{:T(128)}, f32[256]{0:T(256)S(1)}, f32[64,256]{1,0:T(8,128)S(1)}, f32[2,32]{1,0:T(2,128)S(1)}, f32[256]{0:T(256)S(1)}, /*index=5*/f32[4096]{0:...) while((s32[]{:T(128)}, f32[256]{0:T(256)S(1)}, ...), condition=%wide.region_6.7_spmd.clone, body=%wide.region_4.0_spmd.clone.sunk | while | flops 68190488 | bytes 1879617 | solution.py:55
  46.2 0.2 mul.158
  46.5 1.4 %fusion.42 = (f32[256]{0:T(256)S(1)}, bf16[256,512]{0,1:T(8,128)(2,1)S(1)}) fusion(f32[]{:T(128)} %get-tuple-element.752, f32[32,256]{1,0:T(8,128)S(1)} %get-tuple-element.751, f32[32,4096]{1,0:T(8,128)S(1)} %get-tuple-element.750, s32[]{:T(128)S(6)} %select_n.82, f32[512]{0:T(512)S(1)} %dynamic_slice.117, f32[256]{0:T(256)S(1)} %get-tuple-element.748, ...), kind=kOutput, calls=%fused_computation.40.clone.1 | convolution fusion | flops 51379968 | bytes 888840 | tf_op jit(solution)/shard_map/while/body/eval_jaxpr/dot_general | solution.py:36
  47.9 0.2 convolution_add_fusion.4
  48.3 0.2 mul.158
  48.6 1.4 %fusion.42 = (f32[256]{0:T(256)S(1)}, bf16[256,512]{0,1:T(8,128)(2,1)S(1)}) fusion(f32[]{:T(128)} %get-tuple-element.752, f32[32,256]{1,0:T(8,128)S(1)} %get-tuple-element.751, f32[32,4096]{1,0:T(8,128)S(1)} %get-tuple-element.750, s32[]{:T(128)S(6)} %select_n.82, f32[512]{0:T(512)S(1)} %dynamic_slice.117, f32[256]{0:T(256)S(1)} %get-tuple-element.748, ...), kind=kOutput, calls=%fused_computation.40.clone.1 | convolution fusion | flops 51379968 | bytes 888840 | tf_op jit(solution)/shard_map/while/body/eval_jaxpr/dot_general | solution.py:36
  50.0 0.2 convolution_add_fusion.4
  50.4 0.2 mul.158
  50.7 1.4 %fusion.42 = (f32[256]{0:T(256)S(1)}, bf16[256,512]{0,1:T(8,128)(2,1)S(1)}) fusion(f32[]{:T(128)} %get-tuple-element.752, f32[32,256]{1,0:T(8,128)S(1)} %get-tuple-element.751, f32[32,4096]{1,0:T(8,128)S(1)} %get-tuple-element.750, s32[]{:T(128)S(6)} %select_n.82, f32[512]{0:T(512)S(1)} %dynamic_slice.117, f32[256]{0:T(256)S(1)} %get-tuple-element.748, ...), kind=kOutput, calls=%fused_computation.40.clone.1 | convolution fusion | flops 51379968 | bytes 888840 | tf_op jit(solution)/shard_map/while/body/eval_jaxpr/dot_general | solution.py:36
  52.1 0.2 convolution_add_fusion.4
  52.5 0.2 mul.158
  52.8 1.4 %fusion.42 = (f32[256]{0:T(256)S(1)}, bf16[256,512]{0,1:T(8,128)(2,1)S(1)}) fusion(f32[]{:T(128)} %get-tuple-element.752, f32[32,256]{1,0:T(8,128)S(1)} %get-tuple-element.751, f32[32,4096]{1,0:T(8,128)S(1)} %get-tuple-element.750, s32[]{:T(128)S(6)} %select_n.82, f32[512]{0:T(512)S(1)} %dynamic_slice.117, f32[256]{0:T(256)S(1)} %get-tuple-element.748, ...), kind=kOutput, calls=%fused_computation.40.clone.1 | convolution fusion | flops 51379968 | bytes 888840 | tf_op jit(solution)/shard_map/while/body/eval_jaxpr/dot_general | solution.py:36
  54.2 0.2 convolution_add_fusion.4
  54.7 0.2 mul.158
  55.0 1.4 %fusion.42 = (f32[256]{0:T(256)S(1)}, bf16[256,512]{0,1:T(8,128)(2,1)S(1)}) fusion(f32[]{:T(128)} %get-tuple-element.752, f32[32,256]{1,0:T(8,128)S(1)} %get-tuple-element.751, f32[32,4096]{1,0:T(8,128)S(1)} %get-tuple-element.750, s32[]{:T(128)S(6)} %select_n.82, f32[512]{0:T(512)S(1)} %dynamic_slice.117, f32[256]{0:T(256)S(1)} %get-tuple-element.748, ...), kind=kOutput, calls=%fused_computation.40.clone.1 | convolution fusion | flops 51379968 | bytes 888840 | tf_op jit(solution)/shard_map/while/body/eval_jaxpr/dot_general | solution.py:36
  56.4 0.2 convolution_add_fusion.4
  56.8 0.2 mul.158
  57.1 1.4 %fusion.42 = (f32[256]{0:T(256)S(1)}, bf16[256,512]{0,1:T(8,128)(2,1)S(1)}) fusion(f32[]{:T(128)} %get-tuple-element.752, f32[32,256]{1,0:T(8,128)S(1)} %get-tuple-element.751, f32[32,4096]{1,0:T(8,128)S(1)} %get-tuple-element.750, s32[]{:T(128)S(6)} %select_n.82, f32[512]{0:T(512)S(1)} %dynamic_slice.117, f32[256]{0:T(256)S(1)} %get-tuple-element.748, ...), kind=kOutput, calls=%fused_computation.40.clone.1 | convolution fusion | flops 51379968 | bytes 888840 | tf_op jit(solution)/shard_map/while/body/eval_jaxpr/dot_general | solution.py:36
  58.5 0.2 convolution_add_fusion.4
  58.9 0.2 mul.158
  59.2 1.4 %fusion.42 = (f32[256]{0:T(256)S(1)}, bf16[256,512]{0,1:T(8,128)(2,1)S(1)}) fusion(f32[]{:T(128)} %get-tuple-element.752, f32[32,256]{1,0:T(8,128)S(1)} %get-tuple-element.751, f32[32,4096]{1,0:T(8,128)S(1)} %get-tuple-element.750, s32[]{:T(128)S(6)} %select_n.82, f32[512]{0:T(512)S(1)} %dynamic_slice.117, f32[256]{0:T(256)S(1)} %get-tuple-element.748, ...), kind=kOutput, calls=%fused_computation.40.clone.1 | convolution fusion | flops 51379968 | bytes 888840 | tf_op jit(solution)/shard_map/while/body/eval_jaxpr/dot_general | solution.py:36
  60.6 0.2 convolution_add_fusion.4
  61.1 0.2 mul.158
  61.4 1.4 %fusion.42 = (f32[256]{0:T(256)S(1)}, bf16[256,512]{0,1:T(8,128)(2,1)S(1)}) fusion(f32[]{:T(128)} %get-tuple-element.752, f32[32,256]{1,0:T(8,128)S(1)} %get-tuple-element.751, f32[32,4096]{1,0:T(8,128)S(1)} %get-tuple-element.750, s32[]{:T(128)S(6)} %select_n.82, f32[512]{0:T(512)S(1)} %dynamic_slice.117, f32[256]{0:T(256)S(1)} %get-tuple-element.748, ...), kind=kOutput, calls=%fused_computation.40.clone.1 | convolution fusion | flops 51379968 | bytes 888840 | tf_op jit(solution)/shard_map/while/body/eval_jaxpr/dot_general | solution.py:36
  62.8 0.2 convolution_add_fusion.4
  63.0 20.3 %all_gather.23 = bf16[64,4096]{1,0:T(8,128)(2,1)S(1)} all-gather(bf16[64,256]{1,0:T(8,128)(2,1)S(1)} %divide_convert_fusion), channel_id=1, replica_groups=mesh['traj'=16,'tm'=2] {'traj'}, dimensions={1}, use_global_device_ids=true | all-gather | bytes 557056 | tf_op jit(solution)/shard_map/all_gather | solution.py:69
  83.3 0.7 copy-done.4
  84.0 0.6 dynamic-slice
  85.2 0.2 dynamic-update-slice
  85.5 8.0 %all-reduce = s32[32]{0:T(128)S(1)} all-reduce(s32[32]{0:T(128)S(1)} %dynamic-update-slice), channel_id=1, replica_groups=mesh['traj'=16,'tm'=2] {'traj'}, use_global_device_ids=true, to_apply=%add | all-reduce | flops 32 | bytes 256
  93.5 21.6 %all-gather.1 = s32[16,2,24]{2,1,0:T(2,128)S(1)} all-gather(s32[1,2,24]{2,1,0:T(2,128)S(1)} %bitcast.55), channel_id=1, replica_groups=mesh['traj'=16,'tm'=2] {'traj'}, dimensions={0}, use_global_device_ids=true | all-gather | bytes 3264 | tf_op jit(solution)/shard_map/all_gather | solution.py:63
  115.1 0.3 fusion.22
  115.5 15.4 %while.35 = (s32[]{:T(128)}, f32[64,256]{1,0:T(8,128)S(1)}, bf16[64,4096]{1,0:T(8,128)(2,1)S(1)}, f32[32,2]{1,0:T(8,128)S(1)}, f32[4096]{0:T(1024)S(1)}, /*index...) while((s32[]{:T(128)}, f32[64,256]{1,0:T(8,128)S(1)}, ...), condition=%wide.region_8.9_spmd.clone, body=%wide.region_7.8_spmd.clone.sunk | while | flops 68059160 | bytes 1875448 | solution.py:87
  115.5 0.2 mul.162
  115.8 1.4 fusion.47
  117.1 0.2 convolution_add_fusion.5
  117.4 0.2 mul.162
  117.7 1.4 %fusion.47 = bf16[512,256]{1,0:T(8,128)(2,1)S(1)} fusion(f32[32,256]{1,0:T(8,128)S(1)} %get-tuple-element.803, f32[64,8,2,128]{3,2,1,0:T(2,128)S(1)} %bitcast.50, f32[]{:T(128)} %get-tuple-element.804, f32[256]{0:T(256)S(1)} %get-tuple-element.801, f32[512]{0:T(512)S(1)} %dynamic_slice.121, f32[32,4096]{1,0:T(8,128)S(1)} %get-tuple-element.802, ...), kind=kOutput, calls=%fused_computation.21.clone.1 | convolution fusion | flops 51249152 | bytes 887816 | tf_op jit(solution)/shard_map/while/body/eval_jaxpr/dot_general | solution.py:74
  119.1 0.2 convolution_add_fusion.5
  119.3 0.2 mul.162
  119.6 1.4 %fusion.47 = bf16[512,256]{1,0:T(8,128)(2,1)S(1)} fusion(f32[32,256]{1,0:T(8,128)S(1)} %get-tuple-element.803, f32[64,8,2,128]{3,2,1,0:T(2,128)S(1)} %bitcast.50, f32[]{:T(128)} %get-tuple-element.804, f32[256]{0:T(256)S(1)} %get-tuple-element.801, f32[512]{0:T(512)S(1)} %dynamic_slice.121, f32[32,4096]{1,0:T(8,128)S(1)} %get-tuple-element.802, ...), kind=kOutput, calls=%fused_computation.21.clone.1 | convolution fusion | flops 51249152 | bytes 887816 | tf_op jit(solution)/shard_map/while/body/eval_jaxpr/dot_general | solution.py:74
  121.0 0.2 convolution_add_fusion.5
  121.3 0.2 mul.162
  121.6 1.4 fusion.47
  122.9 0.2 convolution_add_fusion.5
  123.2 0.2 mul.162
  123.5 1.4 fusion.47
  124.9 0.2 convolution_add_fusion.5
  125.1 0.2 mul.162
  125.4 1.4 %fusion.47 = bf16[512,256]{1,0:T(8,128)(2,1)S(1)} fusion(f32[32,256]{1,0:T(8,128)S(1)} %get-tuple-element.803, f32[64,8,2,128]{3,2,1,0:T(2,128)S(1)} %bitcast.50, f32[]{:T(128)} %get-tuple-element.804, f32[256]{0:T(256)S(1)} %get-tuple-element.801, f32[512]{0:T(512)S(1)} %dynamic_slice.121, f32[32,4096]{1,0:T(8,128)S(1)} %get-tuple-element.802, ...), kind=kOutput, calls=%fused_computation.21.clone.1 | convolution fusion | flops 51249152 | bytes 887816 | tf_op jit(solution)/shard_map/while/body/eval_jaxpr/dot_general | solution.py:74
  126.8 0.2 convolution_add_fusion.5
  127.1 0.2 mul.162
  127.4 1.4 %fusion.47 = bf16[512,256]{1,0:T(8,128)(2,1)S(1)} fusion(f32[32,256]{1,0:T(8,128)S(1)} %get-tuple-element.803, f32[64,8,2,128]{3,2,1,0:T(2,128)S(1)} %bitcast.50, f32[]{:T(128)} %get-tuple-element.804, f32[256]{0:T(256)S(1)} %get-tuple-element.801, f32[512]{0:T(512)S(1)} %dynamic_slice.121, f32[32,4096]{1,0:T(8,128)S(1)} %get-tuple-element.802, ...), kind=kOutput, calls=%fused_computation.21.clone.1 | convolution fusion | flops 51249152 | bytes 887816 | tf_op jit(solution)/shard_map/while/body/eval_jaxpr/dot_general | solution.py:74
  128.7 0.2 convolution_add_fusion.5
  129.0 0.2 mul.162
  129.3 1.4 fusion.47
  130.7 0.2 convolution_add_fusion.5
  130.9 5.0 %all-gather = f32[128,256]{1,0:T(8,128)S(1)} all-gather(f32[64,256]{1,0:T(8,128)S(1)} %get-tuple-element.472), channel_id=2, replica_groups=mesh['traj'=16,'tm'=2] {'tm'}, dimensions={0}, use_global_device_ids=true | all-gather | bytes 196608 | tf_op jit(solution)/shard_map/all_gather | solution.py:90
  135.9 0.6 reduce_sum.45
  (67 shorter events, 3.3 us)
Async XLA Ops:
  24.8 0.8 copy-start
  24.9 0.8 copy-start.1
  44.5 0.7 copy-start.3
  45.2 0.7 copy-start.2
  83.3 0.7 copy-start.4
